TPU v7x, 256 devices: a whole 4x4x8 slice. The times are simulated.
256 devices in a mesh: row: 8 (over y, x_lo), col: 32 (over z, x_hi, core).
Axes of the slice: x: 4 (x_hi: 2, x_lo: 2; x = x_hi * 2 + x_lo), y: 4, z: 8, core: 2. Of those that a mesh axis runs over, the one named last changes fastest.
Arguments:
- density: bfloat16 [8192, 8192], P('row', 'col'), may hold values from -0.0625 to 0.0625
- density_mask: int32 [64, 64], P('row', 'col'), may hold values from 0 to 1, as said below
- response: bfloat16 [2, 8192, 8192], P(None, 'row', 'col'), may hold values from -6 to 6
- response_mask: int32 [2, 64, 64], P(None, 'row', 'col'), may hold values from 0 to 1, as said below
- filter_mask: int32 [64, 64], P('row', 'col'), may hold values from 0 to 1, as said below
Outputs:
- product: bfloat16 [2, 8192, 8192], P(None, 'row', 'col')
Inputs may be any that keep to these rules, and one draw needn't show every extreme that they name: `density_mask`: diagonal blocks are always nonzero; blocks within cyclic block distance 8 of the diagonal are more often nonzero than blocks further out; whole block rows and whole block columns may be nonzero. `response_mask`: for each direction, diagonal blocks are always nonzero; blocks within cyclic block distance 8 of the diagonal are more often nonzero than blocks further out; whole block rows and whole block columns may be nonzero. `filter_mask`: diagonal blocks are always kept; blocks within cyclic block distance 2 * 8 of the diagonal are more often kept than blocks further out; whole block rows and whole block columns may be kept.
All inputs are finite; a program needn't handle non-finite values.
Results may differ from a plain program's by a relative error of at most 0.001.
Values may be sent and summed in bfloat16 or wider, within the bound.
No kernel may reach another device: no remote copies, remote signals or barrier semaphores. Data moves between devices by JAX's collectives and lax.ppermute only.
A program may use at most 128 MiB of HBM per device.

v0:
```python
import jax
import jax.numpy as jnp
from jax import lax
from jax.sharding import PartitionSpec as P


def in_order(tiles, dim):
    dims = list(tiles.shape[1:])
    dims[dim] *= tiles.shape[0]
    return jnp.moveaxis(tiles, 0, dim).reshape(dims)


def sent_to_all(array, axis):
    peers = lax.axis_size(axis)
    return lax.all_to_all(
        jnp.broadcast_to(array[None], (peers, *array.shape)), axis, 0, 0, tiled=True
    )


def gather_directly(array, axis, dim):
    return in_order(sent_to_all(array, axis), dim)


def expand_blocks(values, mask, blocksize):
    lead = values.shape[:-2]
    height = values.shape[-2] // blocksize
    width = values.shape[-1] // blocksize
    shaped = values.reshape(lead + (height, blocksize, width, blocksize))
    scaled = shaped * mask.astype(values.dtype)[..., :, None, :, None]
    return scaled.reshape(values.shape)


def body(density, density_mask, response, response_mask, filter_mask):
    blocksize = density.shape[1] // density_mask.shape[1]
    masked_density = expand_blocks(density, density_mask, blocksize)
    masked_response = expand_blocks(response, response_mask, blocksize)
    density_full = lax.all_gather(masked_density, "col", axis=1, tiled=True)
    result = jnp.einsum(
        "ik,dkj->dij",
        density_full,
        gather_directly(masked_response, "row", 1),
        preferred_element_type=jnp.float32,
    )
    return expand_blocks(result, filter_mask, blocksize).astype(jnp.bfloat16)


def solution(mesh):
    in_specs = (
        P("row", "col"),
        P("row", "col"),
        P(None, "row", "col"),
        P(None, "row", "col"),
        P("row", "col"),
    )
    out_specs = P(None, "row", "col")
    return jax.shard_map(body, mesh=mesh, in_specs=in_specs, out_specs=out_specs, check_vma=False)
```

profile of v0, /device:TPU:1, one launch (start us, length us, event | category | flops | bytes accessed | tf_op | source)
XLA Modules:
  0.0 235.9 jit_solution(5093998022321355920)
XLA Ops:
  6.5 0.0 all-gather.2.cloned.1.call-start
  6.5 0.7 convert_element_type.13
  7.2 0.1 copy.13
  7.3 0.3 mul.39
  7.7 1.9 bitcast_multiply_fusion.1
  9.6 0.0 all-gather.2.cloned.1.call-update
  9.6 0.7 convert_element_type.12
  10.3 0.1 copy.10
  10.4 0.6 mul.36
  11.0 0.7 mul.37
  11.7 1.5 mul.38
  13.2 0.5 copy.11
  13.8 4.3 %broadcast_in_dim.2 = bf16[8,2,1024,256]{2,3,1,0:T(8,128)(2,1)} broadcast(bf16[2,1024,256]{1,2,0:T(8,128)(2,1)S(1)} %copy.11), dimensions={1,2,3} | broadcast | bytes 9437184 | tf_op jit(solution)/shard_map/broadcast_in_dim | solution.py:16
  18.1 0.0 copy-start
  18.1 6.1 %all-to-all-start = ((bf16[8,2,1024,256]{2,3,1,0:T(8,128)(2,1)}), bf16[8,2,1024,256]{2,3,1,0:T(8,128)(2,1)}, u32[]{:S(2)}, u32[]{:S(2)}) async-start(bf16[8,2,1024,256]{2,3,1,0:T(8,128)(2,1)} %broadcast_in_dim.2), calls=%async_computation | async-start | bytes 16777216 | tf_op jit(solution)/shard_map/all_to_all | solution.py:15
  24.1 0.0 copy-done
  24.1 0.1 mul.42
  24.3 0.2 copy.20
  24.5 136.0 %all-to-all-done = bf16[8,2,1024,256]{2,3,1,0:T(8,128)(2,1)} async-done(((bf16[8,2,1024,256]{2,3,1,0:T(8,128)(2,1)}), bf16[8,2,1024,256]{2,3,1,0:T(8,128)(2,1)}, u32[]{:S(2)}, u32[]{:S(2)}) %all-to-all-start) | async-done | bytes 8388640 | tf_op jit(solution)/shard_map/all_to_all | solution.py:15
  160.5 8.0 %copy.15 = bf16[8,2,32,8,1024]{4,3,0,2,1:T(8,128)(2,1)} copy(bf16[8,2,32,8,1024]{4,3,2,1,0:T(8,128)(2,1)} %bitcast.3) | data formatting | bytes 16777216 | tf_op jit(solution)/shard_map/reshape | solution.py:10
  168.6 44.4 %all-gather.2.cloned.1.call-done = bf16[1024,8192]{1,0:T(8,128)(2,1)} async-done(((bf16[1024,256]{1,0:T(8,128)(2,1)}), bf16[1024,8192]{1,0:T(8,128)(2,1)}) %all-gather.2.cloned.1.call-update) | async-done | bytes 16777232 | tf_op jit(solution)/shard_map/all_gather | solution.py:37
  212.9 14.8 %fusion.2 = bf16[2,1024,256]{1,2,0:T(8,128)(2,1)S(1)} fusion(bf16[2,8192,256]{1,2,0:T(8,128)(2,1)} %bitcast.24, bf16[1024,8192]{1,0:T(8,128)(2,1)} %all-gather.2.cloned.1.call-done, f32[1024,256]{0,1:T(8,128)S(1)} %bitcast.27), kind=kOutput, calls=%fused_computation.3 | convolution fusion | flops 8590983168 | bytes 27262976 | tf_op jit(solution)/shard_map/ik,dkj->dij/dot_general | solution.py:38
  227.8 1.3 copy.14
  (1 shorter events, 0.0 us)
Async XLA Ops:
  6.5 206.4 %all-gather.2.cloned.1.call-start = ((), (), s32[]{:S(2)}) async-start(), calls=%async_computation.1 | async-start | bytes 17301504 | tf_op jit(solution)/shard_map/all_gather | solution.py:37
  18.1 6.1 %copy-start = (s32[8,2]{0,1:T(2,128)S(1)}, s32[8,2]{0,1:T(2,128)}, u32[]{:S(2)}) copy-start(s32[8,2]{0,1:T(2,128)} %param.9) | copy-start | bytes 196
  18.1 142.5 %all-to-all-start = ((bf16[8,2,1024,256]{2,3,1,0:T(8,128)(2,1)}), bf16[8,2,1024,256]{2,3,1,0:T(8,128)(2,1)}, u32[]{:S(2)}, u32[]{:S(2)}) async-start(bf16[8,2,1024,256]{2,3,1,0:T(8,128)(2,1)} %broadcast_in_dim.2), calls=%async_computation | async-start | bytes 16777216 | tf_op jit(solution)/shard_map/all_to_all | solution.py:15
Sparse Core Ops, SparseCore 0:
  9.9 202.9 all-gather.1
where the time goes:
time: 236 us
  waiting for transfers between devices  180 us (76%)
  local copies, waits for them, and re-layouts  16.4 us (7%)
  matrix products  14.8 us (6%)
  between operations  13.5 us (6%)
  starting transfers between devices  6.07 us (3%)
  other arithmetic  4.77 us (2%)
    all_to_all x1, waiting for transfers between devices, sent_to_all(): lax.all_to_all(jnp.broadcast_to(array[None], (peers, *array.shape)), axis...  136 us
    all_gather x1, waiting for transfers between devices, body(): density_full = lax.all_gather(masked_density, 'col', axis=1, tiled=True)  44.4 us
    dot_general x1, matrix products, body(): jnp.einsum('ik,dkj->dij', density_full, gather_directly(masked_response,...  14.8 us
    reshape x1, local copies, waits for them, and re-layouts, in_order(): return jnp.moveaxis(tiles, 0, dim).reshape(dims)  8.04 us
    all_to_all x1, starting transfers between devices, sent_to_all(): lax.all_to_all(jnp.broadcast_to(array[None], (peers, *array.shape)), axis...  6.07 us
  transfers between devices with their start and end apart: 2, of which 2 were waited for; matrix products, arithmetic and copies ran while one was open for 7% of the time, Pallas kernels for 0%

commit v1 on v0

--- a/solution.py
+++ b/solution.py
@@ -34,7 +34,9 @@
     blocksize = density.shape[1] // density_mask.shape[1]
     masked_density = expand_blocks(density, density_mask, blocksize)
     masked_response = expand_blocks(response, response_mask, blocksize)
-    density_full = lax.all_gather(masked_density, "col", axis=1, tiled=True)
+    density_full = jnp.concatenate(
+        lax.all_to_all(jnp.stack([masked_density] * lax.axis_size("col")), "col", 0, 0), axis=1
+    )
     result = jnp.einsum(
         "ik,dkj->dij",
         density_full,

time: 236 us -> 553 us (2.34); the launches traced: 236 us -> 545 us
  waiting for transfers between devices: 180 us -> 442 us
  local copies, waits for them, and re-layouts: 16.4 us -> 65.8 us
  starting transfers between devices: 6.07 us -> 20 us
  between operations: 13.5 us -> 0.11 us
    all_to_all x0 -> x1, waiting for transfers between devices: none -> 350 us  [body(): lax.all_to_all(jnp.stack([masked_density] * lax.axis_size('col')), 'col',...]
    all_gather x1 -> x0, waiting for transfers between devices: 44.4 us -> none  [body(): density_full = lax.all_gather(masked_density, 'col', axis=1, tiled=True)]
    all_to_all x1, waiting for transfers between devices: 136 us -> 91.9 us  [sent_to_all(): lax.all_to_all(jnp.broadcast_to(array[None], (peers, *array.shape)), axis...]
    reshape x0 -> x2, local copies, waits for them, and re-layouts: none -> 43.5 us  [body(): jnp.concatenate(lax.all_to_all(jnp.stack([masked_density] * lax.axis_size...]
    all_to_all x0 -> x1, starting transfers between devices: none -> 14 us  [body(): lax.all_to_all(jnp.stack([masked_density] * lax.axis_size('col')), 'col',...]
    another operation x0 -> x1, local copies, waits for them, and re-layouts: none -> 5.92 us  [body(): jnp.stack([masked_density] * lax.axis_size('col'))]
  transfers between devices with their start and end apart: 2 -> 2, of which waited for: 2 -> 2; matrix products, arithmetic and copies ran while one was open for 7% -> 2% of each run, Pallas kernels for 0% -> 0%
where the time goes in v1:
time: 553 us; the launch traced here: 545 us
  waiting for transfers between devices  442 us (80%)
  local copies, waits for them, and re-layouts  65.8 us (12%)
  starting transfers between devices  20 us (4%)
  matrix products  14.8 us (3%)
    all_to_all x1, waiting for transfers between devices, body(): lax.all_to_all(jnp.stack([masked_density] * lax.axis_size('col')), 'col',...  350 us
    all_to_all x1, waiting for transfers between devices, sent_to_all(): lax.all_to_all(jnp.broadcast_to(array[None], (peers, *array.shape)), axis...  91.9 us
    reshape x2, local copies, waits for them, and re-layouts, body(): jnp.concatenate(lax.all_to_all(jnp.stack([masked_density] * lax.axis_size...  43.5 us
    dot_general x1, matrix products, body(): jnp.einsum('ik,dkj->dij', density_full, gather_directly(masked_response,...  14.8 us
    all_to_all x1, starting transfers between devices, body(): lax.all_to_all(jnp.stack([masked_density] * lax.axis_size('col')), 'col',...  14 us
  transfers between devices with their start and end apart: 2, of which 2 were waited for; matrix products, arithmetic and copies ran while one was open for 2% of the time, Pallas kernels for 0%

profile of v1, /device:TPU:1, one launch (start us, length us, event | category | flops | bytes accessed | tf_op | source)
XLA Modules:
  0.0 545.1 jit_solution(1349697403112684294)
XLA Ops:
  0.0 0.7 convert_element_type.12
  0.7 0.1 copy.10
  0.8 0.6 mul.37
  1.4 0.7 mul.38
  2.1 1.5 mul.39
  3.6 0.5 copy.11
  4.2 4.3 broadcast_in_dim.2
  8.5 6.1 %all-to-all-start = ((bf16[8,2,1024,256]{2,3,1,0:T(8,128)(2,1)}), bf16[8,2,1024,256]{2,3,1,0:T(8,128)(2,1)}, u32[]{:S(2)}, u32[]{:S(2)}) async-start(bf16[8,2,1024,256]{2,3,1,0:T(8,128)(2,1)} %broadcast_in_dim.2), calls=%async_computation | async-start | bytes 16777216 | tf_op jit(solution)/shard_map/all_to_all | solution.py:15
  14.5 0.0 copy-done.2
  14.6 0.1 copy.13
  14.7 0.3 mul.40
  15.0 0.0 copy-done
  15.0 0.1 bitcast_multiply_fusion.1
  15.1 91.9 %all-to-all-done = bf16[8,2,1024,256]{2,3,1,0:T(8,128)(2,1)} async-done(((bf16[8,2,1024,256]{2,3,1,0:T(8,128)(2,1)}), bf16[8,2,1024,256]{2,3,1,0:T(8,128)(2,1)}, u32[]{:S(2)}, u32[]{:S(2)}) %all-to-all-start) | async-done | bytes 8388640 | tf_op jit(solution)/shard_map/all_to_all | solution.py:15
  107.0 5.9 %stack.3 = bf16[32,1024,256]{2,1,0:T(8,128)(2,1)} broadcast(bf16[1024,256]{1,0:T(8,128)(2,1)S(1)} %bitcast_multiply_fusion.1), dimensions={1,2} | broadcast | bytes 17301504 | tf_op jit(solution)/shard_map/stack | solution.py:38
  112.9 14.0 %all-to-all-start.1 = ((bf16[32,1024,256]{2,1,0:T(8,128)(2,1)}), bf16[32,1024,256]{2,1,0:T(8,128)(2,1)}, u32[]{:S(2)}, u32[]{:S(2)}) async-start(bf16[32,1024,256]{2,1,0:T(8,128)(2,1)} %stack.3), calls=%async_computation.1 | async-start | bytes 33554432 | tf_op jit(solution)/shard_map/all_to_all | solution.py:38
  126.9 0.1 mul.43
  127.1 0.2 copy.21
  127.3 8.0 %copy.16 = bf16[8,2,32,8,1024]{4,3,0,2,1:T(8,128)(2,1)} copy(bf16[8,2,32,8,1024]{4,3,2,1,0:T(8,128)(2,1)} %bitcast.3) | data formatting | bytes 16777216 | tf_op jit(solution)/shard_map/reshape | solution.py:10
  135.3 350.2 %all-to-all-done.1 = bf16[32,1024,256]{2,1,0:T(8,128)(2,1)} async-done(((bf16[32,1024,256]{2,1,0:T(8,128)(2,1)}), bf16[32,1024,256]{2,1,0:T(8,128)(2,1)}, u32[]{:S(2)}, u32[]{:S(2)}) %all-to-all-start.1) | async-done | bytes 16777248 | tf_op jit(solution)/shard_map/all_to_all | solution.py:38
  485.5 17.9 %copy.14 = bf16[1024,32,256]{2,1,0:T(8,128)(2,1)} copy(bf16[1024,32,256]{2,0,1:T(8,128)(2,1)} %bitcast.1) | data formatting | bytes 33554432 | tf_op jit(solution)/shard_map/reshape | solution.py:37
  503.4 25.6 %reshape.31 = bf16[1024,8192,1]{1,0,2:T(8,128)(2,1)} reshape(bf16[1024,32,256]{2,1,0:T(8,128)(2,1)} %copy.14) | data formatting | bytes 33554432 | tf_op jit(solution)/shard_map/reshape | solution.py:37
  529.0 14.8 %fusion = bf16[2,1024,256]{1,2,0:T(8,128)(2,1)S(1)} fusion(bf16[2,8192,256]{1,2,0:T(8,128)(2,1)} %bitcast.21, bf16[1024,8192,1]{1,0,2:T(8,128)(2,1)} %reshape.31, f32[1024,256]{0,1:T(8,128)S(1)} %bitcast.24), kind=kOutput, calls=%fused_computation.1 | convolution fusion | flops 8590983168 | bytes 27262976 | tf_op jit(solution)/shard_map/ik,dkj->dij/dot_general | solution.py:40
  543.8 1.3 copy.15
  (6 shorter events, 0.0 us)
Async XLA Ops:
  8.5 6.1 %copy-start.2 = (s32[8,2]{0,1:T(2,128)S(1)}, s32[8,2]{0,1:T(2,128)}, u32[]{:S(2)}) copy-start(s32[8,2]{0,1:T(2,128)} %param.6) | copy-start | bytes 196
  8.5 6.5 %copy-start = (bf16[1024,256]{1,0:T(8,128)(2,1)S(1)}, bf16[1024,256]{1,0:T(8,128)(2,1)}, u32[]{:S(2)}) copy-start(bf16[1024,256]{1,0:T(8,128)(2,1)} %param.5) | copy-start | bytes 1572868
  8.5 98.5 %all-to-all-start = ((bf16[8,2,1024,256]{2,3,1,0:T(8,128)(2,1)}), bf16[8,2,1024,256]{2,3,1,0:T(8,128)(2,1)}, u32[]{:S(2)}, u32[]{:S(2)}) async-start(bf16[8,2,1024,256]{2,3,1,0:T(8,128)(2,1)} %broadcast_in_dim.2), calls=%async_computation | async-start | bytes 16777216 | tf_op jit(solution)/shard_map/all_to_all | solution.py:15
  112.9 14.0 %copy-start.1 = (s32[8,2]{0,1:T(2,128)S(1)}, s32[8,2]{0,1:T(2,128)}, u32[]{:S(2)}) copy-start(s32[8,2]{0,1:T(2,128)} %param.9) | copy-start | bytes 196
  112.9 372.6 %all-to-all-start.1 = ((bf16[32,1024,256]{2,1,0:T(8,128)(2,1)}), bf16[32,1024,256]{2,1,0:T(8,128)(2,1)}, u32[]{:S(2)}, u32[]{:S(2)}) async-start(bf16[32,1024,256]{2,1,0:T(8,128)(2,1)} %stack.3), calls=%async_computation.1 | async-start | bytes 33554432 | tf_op jit(solution)/shard_map/all_to_all | solution.py:38
